TPU v7x, 32 devices: a whole 2x2x4 slice. The times are simulated.
32 devices in a mesh: station: 2 (over x), tm: 16 (over z, y, core).
Axes of the slice: x: 2, y: 2, z: 4, core: 2. Of those that a mesh axis runs over, the one named last changes fastest.
Arguments:
- spectra: float32 [512, 4, 4096], P('tm', 'station'), parts along dimension 1, may hold values from -6 to 6
- synth_taps: float32 [16, 512], replicated, may hold values from -1.5 to 1.5
- analysis_taps: float32 [16, 512], replicated, may hold values from -1.5 to 1.5
Outputs:
- channels: float32 [512, 4, 5120], P('tm', 'station'), parts along dimension 1
There are 2 independent parts, one for each index of `station`. A program takes and returns all parts, laid end to end along the dimension named above; an argument that names none is the same for every part. Nothing has to cross between parts.
All inputs are finite; a program needn't handle non-finite values.
Results may differ from a plain program's by a relative error of at most 0.00007.
Values sent between devices are 32-bit elements; how exact they have to be, the bound alone decides.
No kernel may reach another device: no remote copies, remote signals or barrier semaphores. Data moves between devices by JAX's collectives and lax.ppermute only.
A program may use at most 64 MiB of HBM per device.

v0:
```python
import functools
import math

import jax
import jax.numpy as jnp
import numpy as np
from jax import lax
from jax.experimental import pallas as pl
from jax.experimental.pallas import tpu as pltpu
from jax.sharding import PartitionSpec as P

RT = 32
PHASES = 64
UP, DOWN = 5, 4
LANES = 128
SUB = 8
HALO = 32


def split(value):
    high = value.astype(jnp.bfloat16)
    low = (value - high.astype(jnp.float32)).astype(jnp.bfloat16)
    return high, low


def np_split(value):
    value = value.astype(np.float32)
    high = value.astype(jnp.bfloat16)
    low = (value - high.astype(np.float32)).astype(jnp.bfloat16)
    return high, low


def radix4_tables(width):
    quarter = width // 4
    k = np.arange(quarter)[:, None]
    m = np.arange(quarter)[None, :]
    blocks = []
    for r in range(4):
        angle = ((4 * k + r) * m % width) * (2.0 * math.pi / width)
        cosine = np.cos(angle) / math.sqrt(width)
        sine = np.sin(angle) / math.sqrt(width)
        blocks.append(np.block([[cosine, sine], [-sine, cosine]]))
    return np_split(np.stack(blocks))


def resampler_tables():
    parts = []
    for j in range(UP):
        sample = np.arange(LANES)[None, :] + LANES * j
        start = 128 * (min(j, 3) - 1)
        column = np.arange(2 * LANES)[:, None] + start
        lag = DOWN * sample // UP - column
        phase = PHASES * (DOWN * sample % UP) // UP
        offset = lag + phase / PHASES - (RT // 2 - 1)
        window = 0.5 + 0.5 * np.cos(math.pi * offset / (RT / 2.0))
        coeff = 0.9 * np.sinc(0.9 * offset) * window
        parts.append(np_split(np.where((lag >= 0) & (lag < RT), coeff, 0.0)))
    out = [np.concatenate([high, low], axis=1) for high, low in parts[:3]]
    out.append(np.concatenate([parts[3][0], parts[4][0]], axis=1))
    out.append(np.concatenate([parts[3][1], parts[4][1]], axis=1))
    return np.stack(out)


def lane_iota():
    return lax.broadcasted_iota(jnp.int32, (SUB, LANES), 1)


def prep_kernel(order, blocks, x_ref, o_ref):
    stride = x_ref.shape[0] // (4 * SUB)
    lane = lane_iota()

    def tile(r, k, part):
        return x_ref[pl.ds(r * stride + 2 * k + part, SUB, stride=4 * stride), :]

    for place, dev in enumerate(order):
        for r in range(4):
            for lb in range(blocks):
                for part in range(2):
                    t = (r * blocks + lb) * 2 + part
                    o_ref[place, t * SUB : (t + 1) * SUB, :] = tile(r, blocks * dev + lb, part)
        for part in range(2):
            total = jnp.zeros((SUB, LANES), jnp.float32)
            if dev > 0:
                for r in range(4):
                    value = tile(r, blocks * dev - 1, part)
                    if r < 3:
                        value = pltpu.roll(value, HALO * (r + 1), 1)
                    total = jnp.where(lane // HALO == r, value, total)
            t = 8 * blocks + part
            o_ref[place, t * SUB : (t + 1) * SUB, :] = total


def main_kernel(
    order, frames, x_ref, w_hi, w_lo, res_ref, st_ref, at_ref, o_ref,
    a_ref, v_ref, y_ref, yh_ref, yl_ref, z_ref, u_ref, bh_ref, bl_ref,
):
    blocks = frames // LANES
    count = len(order)
    place_of = {dev: place for place, dev in enumerate(order)}
    f32 = jnp.float32

    def dot(a, b):
        return lax.dot_general(a, b, (((1,), (0,)), ((), ())), preferred_element_type=f32)

    def dot_t(a, b):
        return lax.dot_general(a, b, (((1,), (1,)), ((), ())), preferred_element_type=f32)

    def tile(t):
        return jnp.concatenate(
            [x_ref[place_of[s], t * SUB : (t + 1) * SUB, :] for s in range(count)], axis=0
        )

    halo = [tile(8 * blocks + part).T for part in range(2)]
    for r in range(4):
        rows = [jnp.concatenate([h[r * HALO : (r + 1) * HALO] for h in halo], axis=1)]
        for lb in range(blocks):
            rows.append(
                jnp.concatenate([tile((r * blocks + lb) * 2 + part).T for part in range(2)], axis=1)
            )
        high, low = split(jnp.concatenate(rows, axis=0))
        a_ref[r] = dot(high, w_hi[r]) + dot(low, w_hi[r]) + dot(high, w_lo[r])

    total = frames + HALO

    @pl.loop(0, total // 16)
    def _(i):
        row = pl.ds(pl.multiple_of(i * 16, 16), 16)
        re = [a_ref[r, row, :LANES] for r in range(4)]
        im = [a_ref[r, row, LANES:] for r in range(4)]
        sr, dr = re[0] + re[2], re[0] - re[2]
        si, di = im[0] + im[2], im[0] - im[2]
        tr, er = re[1] + re[3], re[1] - re[3]
        ti, ei = im[1] + im[3], im[1] - im[3]
        v_ref[0, row, :] = sr + tr
        v_ref[4, row, :] = si + ti
        v_ref[1, row, :] = dr - ei
        v_ref[5, row, :] = di + er
        v_ref[2, row, :] = sr - tr
        v_ref[6, row, :] = si - ti
        v_ref[3, row, :] = dr + ei
        v_ref[7, row, :] = di - er

    for k in range(8):
        v_ref[k, total : total + 16, :] = jnp.zeros((16, LANES), f32)
        y_ref[k * 2, 0:SUB, :] = jnp.zeros((SUB, LANES), f32)
        y_ref[k * 2 + 1, 0:SUB, :] = jnp.zeros((SUB, LANES), f32)
        y_ref[16 + k * 2, 0:SUB, :] = jnp.zeros((SUB, LANES), f32)
        y_ref[16 + k * 2 + 1, 0:SUB, :] = jnp.zeros((SUB, LANES), f32)

    taps_len = st_ref.shape[0]
    groups = (total // 4 - 4 + SUB) // SUB
    for q in range(4):
        taps = [
            jnp.broadcast_to(st_ref[p : p + 1, q * LANES : (q + 1) * LANES], (SUB, LANES))
            for p in range(taps_len)
        ]

        @pl.loop(0, 2 * groups)
        def _(i):
            part = i // groups
            t = i - part * groups
            base = t * 32 + 16
            vals = {
                j: v_ref[part * 4 + q, pl.ds(base + j, SUB, stride=4), :]
                for j in range(1 - taps_len, 4)
            }
            for b in range(4):
                acc = taps[0] * vals[b]
                for p in range(1, taps_len):
                    acc = acc + taps[p] * vals[b - p]
                y_ref[part * 16 + b * 4 + q, pl.ds(pl.multiple_of(t * SUB, SUB) + SUB, SUB), :] = acc

    rows = groups * SUB
    both = 2 * rows
    for b in range(4):
        for q in range(4):
            value = jnp.concatenate(
                [y_ref[part * 16 + b * 4 + q, SUB : SUB + rows, :] for part in range(2)], axis=0
            )
            high, low = split(value)
            first = b * both + (both if q == 3 else 0)
            yh_ref[q, first : first + both, :] = high
            yl_ref[q, first : first + both, :] = low
    value = jnp.concatenate(
        [y_ref[part * 16 + 15, SUB - 1 : SUB - 1 + rows, :] for part in range(2)], axis=0
    )
    high, low = split(value)
    yh_ref[3, 0:both, :] = high
    yl_ref[3, 0:both, :] = low

    def store_z(j, value):
        for b in range(4):
            g, q = (5 * b + j) // 4, (5 * b + j) % 4
            for part in range(2):
                first = b * both + part * rows
                z_ref[part * 20 + g * 4 + q] = value[first : first + rows]

    def pair(ref, left, right):
        first = both if left == 2 else 0
        a = ref[3, 0 : 4 * both] if left < 0 else ref[left, 0 : 4 * both]
        return jnp.concatenate([a, ref[right, first if right == 3 else 0 : (first if right == 3 else 0) + 4 * both]], axis=1)

    for j in range(3):
        high = pair(yh_ref, j - 1, j)
        low = pair(yl_ref, j - 1, j)
        wide = dot(high, res_ref[j])
        store_z(j, wide[:, :LANES] + wide[:, LANES:] + dot(low, res_ref[j, :, :LANES]))
    high = pair(yh_ref, 2, 3)
    low = pair(yl_ref, 2, 3)
    wide = dot(high, res_ref[3]) + dot(high, res_ref[4]) + dot(low, res_ref[3])
    store_z(3, wide[:, :LANES])
    store_z(4, wide[:, LANES:])

    outs = frames * UP // DOWN
    taps_len = at_ref.shape[0]
    groups2 = frames // 4 // SUB
    for q in range(4):
        taps = [
            jnp.broadcast_to(at_ref[p : p + 1, q * LANES : (q + 1) * LANES], (SUB, LANES))
            for p in range(taps_len)
        ]

        @pl.loop(0, 2 * groups2)
        def _(i):
            part = i // groups2
            t = i - part * groups2
            vals = {}
            for j in range(1 - taps_len, UP):
                shift = j // UP
                vals[j] = z_ref[part * 20 + (j - UP * shift) * 4 + q, pl.ds(t * SUB + 4 + shift, SUB), :]
            for g in range(UP):
                acc = taps[0] * vals[g]
                for p in range(1, taps_len):
                    acc = acc + taps[p] * vals[g - p]
                u_ref[part * 4 + q, pl.ds(t * SUB * UP + g, SUB, stride=UP), :] = acc

    @pl.loop(0, outs // 16)
    def _(i):
        row = pl.ds(pl.multiple_of(i * 16, 16), 16)
        re = [u_ref[q, row, :] for q in range(4)]
        im = [u_ref[4 + q, row, :] for q in range(4)]
        sr, dr = re[0] + re[2], re[0] - re[2]
        si, di = im[0] + im[2], im[0] - im[2]
        tr, er = re[1] + re[3], re[1] - re[3]
        ti, ei = im[1] + im[3], im[1] - im[3]
        spectra = [
            (sr + tr, si + ti), (dr + ei, di - er), (sr - tr, si - ti), (dr - ei, di + er)
        ]
        for r in range(4):
            for part in range(2):
                high, low = split(spectra[r][part])
                cols = slice(part * LANES, (part + 1) * LANES)
                bh_ref[r, row, cols] = high
                bl_ref[r, row, cols] = low

    lane = lax.broadcasted_iota(jnp.int32, (LANES, LANES), 1)
    full = outs // LANES
    rest = outs - full * LANES
    for r in range(4):
        for ref in (bh_ref, bl_ref):
            ref[r, outs : outs + rest] = ref[r, outs - rest : outs]
        high, low = bh_ref[r], bl_ref[r]
        out = dot_t(w_hi[r], high) + dot_t(w_hi[r], low) + dot_t(w_lo[r], high)
        for part in range(2):
            for k in range(full):
                t = k * SUB + r * 2 + part
                value = out[part * LANES : (part + 1) * LANES, k * LANES : (k + 1) * LANES]
                for place, dev in enumerate(order):
                    o_ref[place, t * SUB : (t + 1) * SUB, :] = value[dev * SUB : (dev + 1) * SUB]
        value = jnp.where(
            lane < rest, out[:LANES, full * LANES :], out[LANES:, full * LANES :]
        )
        t = full * SUB + r
        for place, dev in enumerate(order):
            o_ref[place, t * SUB : (t + 1) * SUB, :] = value[dev * SUB : (dev + 1) * SUB]


def final_kernel(order, x_ref, o_ref):
    stride = o_ref.shape[0] // (4 * SUB)
    lane = lane_iota()
    half = LANES // 2
    place_of = {dev: place for place, dev in enumerate(order)}

    def tile(dev, t):
        return x_ref[place_of[dev], t * SUB : (t + 1) * SUB, :]

    for dev in range(0, len(order), 2):
        for r in range(4):
            for part in range(2):
                t = r * 2 + part
                ends = [tile(dev, 16 + r), tile(dev + 1, 16 + r)]
                ends[1 - part] = pltpu.roll(ends[1 - part], half, 1)
                r0 = pltpu.roll(tile(dev + 1, t), half, 1)
                r1 = pltpu.roll(tile(dev + 1, 8 + t), half, 1)
                values = [
                    tile(dev, t),
                    tile(dev, 8 + t),
                    jnp.where(lane < half, ends[0], r0),
                    jnp.where(lane < half, r0, r1),
                    jnp.where(lane < half, r1, ends[1]),
                ]
                for k, value in enumerate(values):
                    first = r * stride + (5 * (dev // 2) + k) * 2 + part
                    o_ref[pl.ds(first, SUB, stride=4 * stride), :] = value


def shards(order, spectra, synth_taps, analysis_taps):
    count = lax.axis_size("tm")
    channels, parts, length = spectra.shape
    width = channels * count
    frames = length // count
    outs = frames * UP // DOWN
    blocks = frames // LANES
    order = tuple(order)
    groups = [list(order)]
    tiled = channels == 4 * SUB
    vmem = pl.BlockSpec(memory_space=pltpu.VMEM)
    f32, bf16 = jnp.float32, jnp.bfloat16
    rows_in = 8 * blocks * SUB + 2 * SUB
    rows_out = (outs * 64) // LANES
    sub = channels // 4

    def exchange(value):
        return lax.all_to_all(
            value, "tm", split_axis=0, concat_axis=0, tiled=True, axis_index_groups=groups
        )

    if tiled:
        flat = spectra.reshape(channels, 2, length // LANES, LANES).transpose(0, 2, 1, 3)
        flat = flat.reshape(-1, LANES)
        sent = pl.pallas_call(
            functools.partial(prep_kernel, order, blocks),
            out_shape=jax.ShapeDtypeStruct((count, rows_in, LANES), f32),
            in_specs=[vmem],
            out_specs=vmem,
        )(flat)
        received = exchange(sent)
        inner = order
    else:
        cut = spectra.reshape(sub, 4, 2, count, blocks, LANES).transpose(3, 1, 4, 2, 0, 5)
        tail = spectra.reshape(sub, 4, 2, count, frames)[..., frames - HALO :]
        tail = jnp.concatenate([jnp.zeros_like(tail[..., :1, :]), tail[..., :-1, :]], axis=3)
        tail = tail.transpose(3, 2, 0, 1, 4).reshape(count, 2 * sub, LANES)
        sent = jnp.concatenate([cut.reshape(count, 8 * blocks * sub, LANES), tail], axis=1)
        received = exchange(sent[np.array(order)])
        received = received[np.argsort(np.array(order))]
        tiles = 8 * blocks + 2
        inner = tuple(range(width // 4 // SUB))
        received = received.reshape(count, tiles, sub, LANES).transpose(1, 0, 2, 3)
        received = received.reshape(tiles, len(inner), SUB, LANES).transpose(1, 0, 2, 3)
        received = received.reshape(len(inner), tiles * SUB, LANES)

    w_hi, w_lo = radix4_tables(width)
    res = resampler_tables()
    rows = ((frames + HALO) // 4 - 4 + SUB) // SUB * SUB
    made = pl.pallas_call(
        functools.partial(main_kernel, inner, frames),
        out_shape=jax.ShapeDtypeStruct((len(inner), rows_out, LANES), f32),
        in_specs=[vmem] * 6,
        out_specs=vmem,
        scratch_shapes=[
            pltpu.VMEM((4, frames + HALO, 2 * LANES), f32),
            pltpu.VMEM((8, frames + HALO + 16, LANES), f32),
            pltpu.VMEM((32, rows + SUB, LANES), f32),
            pltpu.VMEM((4, 10 * rows, LANES), bf16),
            pltpu.VMEM((4, 10 * rows, LANES), bf16),
            pltpu.VMEM((40, rows, LANES), f32),
            pltpu.VMEM((8, outs, LANES), f32),
            pltpu.VMEM((4, outs + outs % LANES, 2 * LANES), bf16),
            pltpu.VMEM((4, outs + outs % LANES, 2 * LANES), bf16),
        ],
    )(received, w_hi, w_lo, res, synth_taps, analysis_taps)

    if tiled:
        back = exchange(made)
        out = pl.pallas_call(
            functools.partial(final_kernel, order),
            out_shape=jax.ShapeDtypeStruct((channels * 2 * count * outs // LANES, LANES), f32),
            in_specs=[vmem],
            out_specs=vmem,
        )(back)
        out = out.reshape(channels, count * outs // LANES, 2, LANES).transpose(0, 2, 1, 3)
        return out.reshape(channels, 2, count * outs)
    tiles = rows_out // SUB
    made = made.reshape(len(inner), tiles, SUB, LANES).transpose(1, 0, 2, 3)
    made = made.reshape(tiles, count, sub, LANES).transpose(1, 0, 2, 3)
    back = exchange(made[np.array(order)])
    back = back[np.argsort(np.array(order))]
    full = outs // LANES
    head = back[:, : 8 * full].reshape(count, full, 4, 2, sub, LANES).transpose(4, 2, 3, 0, 1, 5)
    head = head.reshape(channels, 2, count, full * LANES)
    rest = back[:, 8 * full :].reshape(count, 4, sub, 2, outs - full * LANES).transpose(2, 1, 3, 0, 4)
    rest = rest.reshape(channels, 2, count, -1)
    return jnp.concatenate([head, rest], axis=3).reshape(channels, 2, count * outs)


def solution(mesh):
    in_specs = (P("tm", "station", None), P(), P())
    out_specs = P("tm", "station", None)
    order = list(range(mesh.shape["tm"]))[::-1]
    return jax.shard_map(
        functools.partial(shards, order),
        mesh=mesh,
        in_specs=in_specs,
        out_specs=out_specs,
        check_vma=False,
    )
```

profile of v0, /device:TPU:0, one launch (start us, length us, event | category | flops | bytes accessed | tf_op | source)
XLA Modules:
  0.0 90.6 jit_solution(6390349348770579650)
XLA Ops:
  0.0 3.1 %shard_map.64 = f32[16,144,128]{2,1,0:T(8,128)} custom-call(f32[2048,128]{1,0:T(8,128)} %bitcast.10), custom_call_target="tpu_custom_call" | custom-call | tf_op jit(solution)/shard_map/pallas_call | solution.py:331
  3.1 36.4 %all_to_all.10.x_ref = f32[16,144,128]{2,1,0:T(8,128)} all-to-all(f32[16,144,128]{2,1,0:T(8,128)} %shard_map.64), channel_id=1, replica_groups={{15,14,13,12,11,10,9,8,7,6,5,4,3,2,1,0},{31,30,29,28,27,26,25,24,23,22,..., dimensions={0} | all-to-all | bytes 2359296 | tf_op jit(solution)/shard_map/all_to_all | solution.py:324
  39.5 11.6 %shard_map.65 = f32[16,160,128]{2,1,0:T(8,128)} custom-call(f32[16,144,128]{2,1,0:T(8,128)} %all_to_all.10.x_ref, bf16[4,256,256]{2,1,0:T(8,128)(2,1)} %constant.6.clone.w_hi, bf16[4,256,256]{2,1,0:T(8,128)(2,1)} %constant.7.clone.w_lo, bf16[5,256,256]{2,1,0:T(8,128)(2,1)} %constant.8.clone.res_ref, f32[16,512]{1,0:T(8,128)} %st_ref.1, f32[16,512]{1,0:T(8,128)} %at_ref.1), custom_call_target="tpu_custom_call" | custom-call | tf_op jit(solution)/shard_map/pallas_call | solution.py:356
  51.1 36.3 %all_to_all.11.x_ref = f32[16,160,128]{2,1,0:T(8,128)} all-to-all(f32[16,160,128]{2,1,0:T(8,128)} %shard_map.65), channel_id=1, replica_groups={{15,14,13,12,11,10,9,8,7,6,5,4,3,2,1,0},{31,30,29,28,27,26,25,24,23,22,..., dimensions={0} | all-to-all | bytes 2621440 | tf_op jit(solution)/shard_map/all_to_all | solution.py:324
  87.3 3.2 %shard_map.66 = f32[2560,128]{1,0:T(8,128)} custom-call(f32[16,160,128]{2,1,0:T(8,128)} %all_to_all.11.x_ref), custom_call_target="tpu_custom_call" | custom-call | tf_op jit(solution)/shard_map/pallas_call | solution.py:376
where the time goes:
time: 90.9 us; the launch traced here: 90.6 us
  blocking collectives  72.6 us (80%)
  Pallas kernels  17.9 us (20%)
    all_to_all x2, blocking collectives, exchange(): lax.all_to_all(value, 'tm', split_axis=0, concat_axis=0, tiled=True, axis...  72.6 us
    pallas_call x1, Pallas kernels, shards(): pl.pallas_call(functools.partial(main_kernel, inner, frames), out_shape=j...  11.6 us
    pallas_call x1, Pallas kernels, shards(): pl.pallas_call(functools.partial(final_kernel, order), out_shape=jax.Shap...  3.22 us
    pallas_call x1, Pallas kernels, shards(): pl.pallas_call(functools.partial(prep_kernel, order, blocks), out_shape=j...  3.11 us

commit v1 on v0

--- a/solution.py
+++ b/solution.py
@@ -14,6 +14,7 @@
 UP, DOWN = 5, 4
 LANES = 128
 SUB = 8
+ORDER = [5, 2, 7, 13, 12, 11, 0, 4, 8, 15, 6, 14, 10, 3, 9, 1]
 HALO = 32
 
 
@@ -150,25 +151,32 @@
     taps_len = st_ref.shape[0]
     groups = (total // 4 - 4 + SUB) // SUB
     for q in range(4):
-        taps = [
-            jnp.broadcast_to(st_ref[p : p + 1, q * LANES : (q + 1) * LANES], (SUB, LANES))
-            for p in range(taps_len)
-        ]
-
-        @pl.loop(0, 2 * groups)
-        def _(i):
-            part = i // groups
-            t = i - part * groups
+
+        @pl.loop(0, groups)
+        def _(t):
             base = t * 32 + 16
-            vals = {
-                j: v_ref[part * 4 + q, pl.ds(base + j, SUB, stride=4), :]
-                for j in range(1 - taps_len, 4)
-            }
-            for b in range(4):
-                acc = taps[0] * vals[b]
-                for p in range(1, taps_len):
-                    acc = acc + taps[p] * vals[b - p]
-                y_ref[part * 16 + b * 4 + q, pl.ds(pl.multiple_of(t * SUB, SUB) + SUB, SUB), :] = acc
+            accs = {}
+            vals = {}
+
+            def load(part, j):
+                vals[part, j] = v_ref[part * 4 + q, pl.ds(base + j, SUB, stride=4), :]
+
+            for part in range(2):
+                for j in range(1, 4):
+                    load(part, j)
+            for p in range(taps_len):
+                tap = jnp.broadcast_to(
+                    st_ref[p : p + 1, q * LANES : (q + 1) * LANES], (SUB, LANES)
+                )
+                for part in range(2):
+                    load(part, -p)
+                    for b in range(4):
+                        term = tap * vals[part, b - p]
+                        accs[part, b] = term if p == 0 else accs[part, b] + term
+            for part in range(2):
+                for b in range(4):
+                    row = pl.ds(pl.multiple_of(t * SUB, SUB) + SUB, SUB)
+                    y_ref[part * 16 + b * 4 + q, row, :] = accs[part, b]
 
     rows = groups * SUB
     both = 2 * rows
@@ -215,24 +223,33 @@
     taps_len = at_ref.shape[0]
     groups2 = frames // 4 // SUB
     for q in range(4):
-        taps = [
-            jnp.broadcast_to(at_ref[p : p + 1, q * LANES : (q + 1) * LANES], (SUB, LANES))
-            for p in range(taps_len)
-        ]
-
-        @pl.loop(0, 2 * groups2)
-        def _(i):
-            part = i // groups2
-            t = i - part * groups2
+
+        @pl.loop(0, groups2)
+        def _(t):
+            accs = {}
             vals = {}
-            for j in range(1 - taps_len, UP):
+
+            def load(part, j):
                 shift = j // UP
-                vals[j] = z_ref[part * 20 + (j - UP * shift) * 4 + q, pl.ds(t * SUB + 4 + shift, SUB), :]
-            for g in range(UP):
-                acc = taps[0] * vals[g]
-                for p in range(1, taps_len):
-                    acc = acc + taps[p] * vals[g - p]
-                u_ref[part * 4 + q, pl.ds(t * SUB * UP + g, SUB, stride=UP), :] = acc
+                slot = part * 20 + (j - UP * shift) * 4 + q
+                vals[part, j] = z_ref[slot, pl.ds(t * SUB + 4 + shift, SUB), :]
+
+            for part in range(2):
+                for j in range(1, UP):
+                    load(part, j)
+            for p in range(taps_len):
+                tap = jnp.broadcast_to(
+                    at_ref[p : p + 1, q * LANES : (q + 1) * LANES], (SUB, LANES)
+                )
+                for part in range(2):
+                    load(part, -p)
+                    for g in range(UP):
+                        term = tap * vals[part, g - p]
+                        accs[part, g] = term if p == 0 else accs[part, g] + term
+            for part in range(2):
+                for g in range(UP):
+                    row = pl.ds(t * SUB * UP + g, SUB, stride=UP)
+                    u_ref[part * 4 + q, row, :] = accs[part, g]
 
     @pl.loop(0, outs // 16)
     def _(i):
@@ -257,19 +274,25 @@
     full = outs // LANES
     rest = outs - full * LANES
     for r in range(4):
-        for ref in (bh_ref, bl_ref):
-            ref[r, outs : outs + rest] = ref[r, outs - rest : outs]
-        high, low = bh_ref[r], bl_ref[r]
+        for place in range(2):
+            first = full * LANES + place * rest
+            last = slice(full * LANES, full * LANES + rest)
+            if place == 1:
+                bh_ref[r, first : first + rest] = bh_ref[r, last]
+            bh_ref[r, first + LANES : first + LANES + rest] = bl_ref[r, last]
+        main = slice(0, full * LANES)
+        high, low = bh_ref[r, main], bl_ref[r, main]
         out = dot_t(w_hi[r], high) + dot_t(w_hi[r], low) + dot_t(w_lo[r], high)
+        tail = dot_t(w_hi[r], bh_ref[r, full * LANES :])
+        tail = tail[:, :LANES] + tail[:, LANES:]
+        tail = tail + dot_t(w_lo[r], bh_ref[r, full * LANES : (full + 1) * LANES])
         for part in range(2):
             for k in range(full):
                 t = k * SUB + r * 2 + part
                 value = out[part * LANES : (part + 1) * LANES, k * LANES : (k + 1) * LANES]
                 for place, dev in enumerate(order):
                     o_ref[place, t * SUB : (t + 1) * SUB, :] = value[dev * SUB : (dev + 1) * SUB]
-        value = jnp.where(
-            lane < rest, out[:LANES, full * LANES :], out[LANES:, full * LANES :]
-        )
+        value = jnp.where(lane < rest, tail[:LANES], tail[LANES:])
         t = full * SUB + r
         for place, dev in enumerate(order):
             o_ref[place, t * SUB : (t + 1) * SUB, :] = value[dev * SUB : (dev + 1) * SUB]
@@ -319,6 +342,7 @@
     rows_in = 8 * blocks * SUB + 2 * SUB
     rows_out = (outs * 64) // LANES
     sub = channels // 4
+    small = pltpu.CompilerParams(vmem_limit_bytes=8 << 20)
 
     def exchange(value):
         return lax.all_to_all(
@@ -333,6 +357,7 @@
             out_shape=jax.ShapeDtypeStruct((count, rows_in, LANES), f32),
             in_specs=[vmem],
             out_specs=vmem,
+            compiler_params=small,
         )(flat)
         received = exchange(sent)
         inner = order
@@ -366,9 +391,10 @@
             pltpu.VMEM((4, 10 * rows, LANES), bf16),
             pltpu.VMEM((40, rows, LANES), f32),
             pltpu.VMEM((8, outs, LANES), f32),
-            pltpu.VMEM((4, outs + outs % LANES, 2 * LANES), bf16),
-            pltpu.VMEM((4, outs + outs % LANES, 2 * LANES), bf16),
+            pltpu.VMEM((4, outs + 3 * (outs % LANES), 2 * LANES), bf16),
+            pltpu.VMEM((4, outs, 2 * LANES), bf16),
         ],
+        compiler_params=pltpu.CompilerParams(vmem_limit_bytes=24 << 20),
     )(received, w_hi, w_lo, res, synth_taps, analysis_taps)
 
     if tiled:
@@ -378,6 +404,7 @@
             out_shape=jax.ShapeDtypeStruct((channels * 2 * count * outs // LANES, LANES), f32),
             in_specs=[vmem],
             out_specs=vmem,
+            compiler_params=small,
         )(back)
         out = out.reshape(channels, count * outs // LANES, 2, LANES).transpose(0, 2, 1, 3)
         return out.reshape(channels, 2, count * outs)
@@ -397,7 +424,9 @@
 def solution(mesh):
     in_specs = (P("tm", "station", None), P(), P())
     out_specs = P("tm", "station", None)
-    order = list(range(mesh.shape["tm"]))[::-1]
+    order = list(range(mesh.shape["tm"]))
+    if len(order) == len(ORDER):
+        order = ORDER
     return jax.shard_map(
         functools.partial(shards, order),
         mesh=mesh,

time: 90.9 us -> 80.9 us (0.89)
  Pallas kernels: 17.9 us -> 9.64 us
  blocking collectives: 72.6 us -> 69.5 us
  local copies, waits for them, and re-layouts: 0 us -> 1.26 us
    pallas_call x1, Pallas kernels: 11.6 us -> 6.85 us  [shards(): pl.pallas_call(functools.partial(main_kernel, inner, frames), out_shape=j...]
    all_to_all x2, blocking collectives: 72.6 us -> 69.5 us  [exchange(): lax.all_to_all(value, 'tm', split_axis=0, concat_axis=0, tiled=True, axis...]
    pallas_call x1, Pallas kernels: 3.11 us -> 0.87 us  [shards(): pl.pallas_call(functools.partial(prep_kernel, order, blocks), out_shape=j...]
    pallas_call x1, Pallas kernels: 3.22 us -> 1.92 us  [shards(): pl.pallas_call(functools.partial(final_kernel, order), out_shape=jax.Shap...]
    unnamed x0 -> x12, local copies, waits for them, and re-layouts: none -> 1.26 us
where the time goes in v1:
time: 80.9 us; the launch traced here: 80.5 us
  blocking collectives  69.5 us (86%)
  Pallas kernels  9.64 us (12%)
  local copies, waits for them, and re-layouts  1.26 us (2%)
    all_to_all x2, blocking collectives, exchange(): lax.all_to_all(value, 'tm', split_axis=0, concat_axis=0, tiled=True, axis...  69.5 us
    pallas_call x1, Pallas kernels, shards(): pl.pallas_call(functools.partial(main_kernel, inner, frames), out_shape=j...  6.85 us
    pallas_call x1, Pallas kernels, shards(): pl.pallas_call(functools.partial(final_kernel, order), out_shape=jax.Shap...  1.92 us

profile of v1, /device:TPU:0, one launch (start us, length us, event | category | flops | bytes accessed | tf_op | source)
XLA Modules:
  0.0 80.5 jit_solution(2497922754489965901)
XLA Ops:
  0.0 0.0 copy-start
  0.0 1.2 %copy-done = f32[32,2,4096]{2,1,0:T(2,128)S(1)} copy-done((f32[32,2,4096]{2,1,0:T(2,128)S(1)}, f32[32,2,4096]{2,1,0:T(2,128)}, u32[]{:S(2)}) %copy-start) | copy-done | bytes 1048600
  1.2 0.9 %shard_map.64 = f32[16,144,128]{2,1,0:T(8,128)S(1)} custom-call(f32[2048,128]{1,0:T(8,128)S(1)} %bitcast.10), custom_call_target="tpu_custom_call" | custom-call | tf_op jit(solution)/shard_map/pallas_call | solution.py:355
  2.1 0.0 copy-start.1
  2.1 0.0 copy-start.2
  2.1 0.0 copy-start.3
  2.1 0.0 copy-start.4
  2.2 0.0 copy-start.5
  2.2 35.9 %all_to_all.10.x_ref = f32[16,144,128]{2,1,0:T(8,128)S(1)} all-to-all(f32[16,144,128]{2,1,0:T(8,128)S(1)} %shard_map.64), channel_id=1, replica_groups={{5,2,7,13,12,11,0,4,8,15,6,14,10,3,9,1},{21,18,23,29,28,27,16,20,24,31,..., dimensions={0} | all-to-all | bytes 2359296 | tf_op jit(solution)/shard_map/all_to_all | solution.py:348
  38.1 0.0 copy-done.1
  38.1 0.0 copy-done.2
  38.1 0.0 copy-done.3
  38.1 0.0 copy-done.4
  38.1 0.0 copy-done.5
  38.1 6.8 %shard_map.65 = f32[16,160,128]{2,1,0:T(8,128)S(1)} custom-call(f32[16,144,128]{2,1,0:T(8,128)S(1)} %all_to_all.10.x_ref, bf16[4,256,256]{2,1,0:T(8,128)(2,1)S(1)} %copy-done.3, bf16[4,256,256]{2,1,0:T(8,128)(2,1)S(1)} %copy-done.2, bf16[5,256,256]{2,1,0:T(8,128)(2,1)S(1)} %copy-done.1, f32[16,512]{1,0:T(8,128)S(1)} %copy-done.4, f32[16,512]{1,0:T(8,128)S(1)} %copy-done.5), custom_call_target="tpu_custom_call" | custom-call | tf_op jit(solution)/shard_map/pallas_call | solution.py:381
  45.0 33.6 %all_to_all.11.x_ref = f32[16,160,128]{2,1,0:T(8,128)S(1)} all-to-all(f32[16,160,128]{2,1,0:T(8,128)S(1)} %shard_map.65), channel_id=1, replica_groups={{5,2,7,13,12,11,0,4,8,15,6,14,10,3,9,1},{21,18,23,29,28,27,16,20,24,31,..., dimensions={0} | all-to-all | bytes 2621440 | tf_op jit(solution)/shard_map/all_to_all | solution.py:348
  78.6 1.9 %shard_map.66 = f32[2560,128]{1,0:T(8,128)} custom-call(f32[16,160,128]{2,1,0:T(8,128)S(1)} %all_to_all.11.x_ref), custom_call_target="tpu_custom_call" | custom-call | tf_op jit(solution)/shard_map/pallas_call | solution.py:402
Async XLA Ops:
  0.0 1.2 %copy-start = (f32[32,2,4096]{2,1,0:T(2,128)S(1)}, f32[32,2,4096]{2,1,0:T(2,128)}, u32[]{:S(2)}) copy-start(f32[32,2,4096]{2,1,0:T(2,128)} %param.6) | copy-start | bytes 3145732
  2.1 36.0 %copy-start.1 = (bf16[5,256,256]{2,1,0:T(8,128)(2,1)S(1)}, bf16[5,256,256]{2,1,0:T(8,128)(2,1)}, u32[]{:S(2)}) copy-start(bf16[5,256,256]{2,1,0:T(8,128)(2,1)} %constant.8.clone.res_ref) | copy-start | bytes 1966084
  2.1 36.0 %copy-start.2 = (bf16[4,256,256]{2,1,0:T(8,128)(2,1)S(1)}, bf16[4,256,256]{2,1,0:T(8,128)(2,1)}, u32[]{:S(2)}) copy-start(bf16[4,256,256]{2,1,0:T(8,128)(2,1)} %constant.7.clone.w_lo) | copy-start | bytes 1572868
  2.1 35.9 %copy-start.3 = (bf16[4,256,256]{2,1,0:T(8,128)(2,1)S(1)}, bf16[4,256,256]{2,1,0:T(8,128)(2,1)}, u32[]{:S(2)}) copy-start(bf16[4,256,256]{2,1,0:T(8,128)(2,1)} %constant.6.clone.w_hi) | copy-start | bytes 1572868
  2.1 35.9 %copy-start.4 = (f32[16,512]{1,0:T(8,128)S(1)}, f32[16,512]{1,0:T(8,128)}, u32[]{:S(2)}) copy-start(f32[16,512]{1,0:T(8,128)} %st_ref.1) | copy-start | bytes 98308
  2.2 35.9 %copy-start.5 = (f32[16,512]{1,0:T(8,128)S(1)}, f32[16,512]{1,0:T(8,128)}, u32[]{:S(2)}) copy-start(f32[16,512]{1,0:T(8,128)} %at_ref.1) | copy-start | bytes 98308

commit v2 on v1

--- a/solution.py
+++ b/solution.py
@@ -15,6 +15,7 @@
 LANES = 128
 SUB = 8
 ORDER = [5, 2, 7, 13, 12, 11, 0, 4, 8, 15, 6, 14, 10, 3, 9, 1]
+PREP_VMEM = 8 << 20
 HALO = 32
 
 
@@ -66,24 +67,33 @@
     return lax.broadcasted_iota(jnp.int32, (SUB, LANES), 1)
 
 
-def prep_kernel(order, blocks, x_ref, o_ref):
-    stride = x_ref.shape[0] // (4 * SUB)
+def prep_kernel(order, blocks, x_ref, o_ref, buf_ref, sems):
+    sub, _, length, _ = x_ref.shape
     lane = lane_iota()
-
-    def tile(r, k, part):
-        return x_ref[pl.ds(r * stride + 2 * k + part, SUB, stride=4 * stride), :]
-
-    for place, dev in enumerate(order):
-        for r in range(4):
+    copies = [
+        pltpu.make_async_copy(x_ref.at[:, r], buf_ref.at[r], sems.at[r]) for r in range(4)
+    ]
+    for copy in copies:
+        copy.start()
+    for r in range(4):
+        copies[r].wait()
+        flat_ref = buf_ref.at[r].reshape(sub * length, LANES)
+        for place, dev in enumerate(order):
             for lb in range(blocks):
                 for part in range(2):
                     t = (r * blocks + lb) * 2 + part
-                    o_ref[place, t * SUB : (t + 1) * SUB, :] = tile(r, blocks * dev + lb, part)
+                    row = 2 * (blocks * dev + lb) + part
+                    o_ref[place, t * SUB : (t + 1) * SUB, :] = flat_ref[
+                        pl.ds(row, SUB, stride=length), :
+                    ]
+    for place, dev in enumerate(order):
         for part in range(2):
             total = jnp.zeros((SUB, LANES), jnp.float32)
             if dev > 0:
+                last = order.index(dev - 1)
                 for r in range(4):
-                    value = tile(r, blocks * dev - 1, part)
+                    t = (r * blocks + blocks - 1) * 2 + part
+                    value = o_ref[last, t * SUB : (t + 1) * SUB, :]
                     if r < 3:
                         value = pltpu.roll(value, HALO * (r + 1), 1)
                     total = jnp.where(lane // HALO == r, value, total)
@@ -152,7 +162,7 @@
     groups = (total // 4 - 4 + SUB) // SUB
     for q in range(4):
 
-        @pl.loop(0, groups)
+        @pl.loop(0, groups, unroll=3)
         def _(t):
             base = t * 32 + 16
             accs = {}
@@ -224,7 +234,7 @@
     groups2 = frames // 4 // SUB
     for q in range(4):
 
-        @pl.loop(0, groups2)
+        @pl.loop(0, groups2, unroll=2)
         def _(t):
             accs = {}
             vals = {}
@@ -298,17 +308,19 @@
             o_ref[place, t * SUB : (t + 1) * SUB, :] = value[dev * SUB : (dev + 1) * SUB]
 
 
-def final_kernel(order, x_ref, o_ref):
-    stride = o_ref.shape[0] // (4 * SUB)
+def final_kernel(order, x_ref, o_ref, buf_ref, sems):
+    _, _, length, _ = o_ref.shape
     lane = lane_iota()
     half = LANES // 2
     place_of = {dev: place for place, dev in enumerate(order)}
+    copies = []
 
     def tile(dev, t):
         return x_ref[place_of[dev], t * SUB : (t + 1) * SUB, :]
 
-    for dev in range(0, len(order), 2):
-        for r in range(4):
+    for r in range(4):
+        flat_ref = buf_ref.at[r].reshape(SUB * length, LANES)
+        for dev in range(0, len(order), 2):
             for part in range(2):
                 t = r * 2 + part
                 ends = [tile(dev, 16 + r), tile(dev + 1, 16 + r)]
@@ -323,8 +335,12 @@
                     jnp.where(lane < half, r1, ends[1]),
                 ]
                 for k, value in enumerate(values):
-                    first = r * stride + (5 * (dev // 2) + k) * 2 + part
-                    o_ref[pl.ds(first, SUB, stride=4 * stride), :] = value
+                    first = (5 * (dev // 2) + k) * 2 + part
+                    flat_ref[pl.ds(first, SUB, stride=length), :] = value
+        copies.append(pltpu.make_async_copy(buf_ref.at[r], o_ref.at[:, r], sems.at[r]))
+        copies[-1].start()
+    for copy in copies:
+        copy.wait()
 
 
 def shards(order, spectra, synth_taps, analysis_taps):
@@ -338,6 +354,7 @@
     groups = [list(order)]
     tiled = channels == 4 * SUB
     vmem = pl.BlockSpec(memory_space=pltpu.VMEM)
+    hbm = pl.BlockSpec(memory_space=pltpu.HBM)
     f32, bf16 = jnp.float32, jnp.bfloat16
     rows_in = 8 * blocks * SUB + 2 * SUB
     rows_out = (outs * 64) // LANES
@@ -351,13 +368,18 @@
 
     if tiled:
         flat = spectra.reshape(channels, 2, length // LANES, LANES).transpose(0, 2, 1, 3)
-        flat = flat.reshape(-1, LANES)
+        flat = flat.reshape(sub, 4, -1, LANES)
+        flat = pltpu.with_memory_space_constraint(flat, pltpu.HBM)
         sent = pl.pallas_call(
             functools.partial(prep_kernel, order, blocks),
             out_shape=jax.ShapeDtypeStruct((count, rows_in, LANES), f32),
-            in_specs=[vmem],
+            in_specs=[hbm],
             out_specs=vmem,
-            compiler_params=small,
+            scratch_shapes=[
+                pltpu.VMEM((4, sub) + flat.shape[2:], f32),
+                pltpu.SemaphoreType.DMA((4,)),
+            ],
+            compiler_params=pltpu.CompilerParams(vmem_limit_bytes=PREP_VMEM),
         )(flat)
         received = exchange(sent)
         inner = order
@@ -401,9 +423,13 @@
         back = exchange(made)
         out = pl.pallas_call(
             functools.partial(final_kernel, order),
-            out_shape=jax.ShapeDtypeStruct((channels * 2 * count * outs // LANES, LANES), f32),
+            out_shape=jax.ShapeDtypeStruct((sub, 4, 2 * count * outs // LANES, LANES), f32),
             in_specs=[vmem],
-            out_specs=vmem,
+            out_specs=hbm,
+            scratch_shapes=[
+                pltpu.VMEM((4, sub, 2 * count * outs // LANES, LANES), f32),
+                pltpu.SemaphoreType.DMA((4,)),
+            ],
             compiler_params=small,
         )(back)
         out = out.reshape(channels, count * outs // LANES, 2, LANES).transpose(0, 2, 1, 3)

time: 80.9 us -> 79.3 us (0.980)
  local copies, waits for them, and re-layouts: 1.26 us -> 0.03 us
    unnamed x12 -> x10, local copies, waits for them, and re-layouts: 1.26 us -> 0.03 us
    pallas_call x1, Pallas kernels: 0.87 us -> 1.7 us  [shards(): pl.pallas_call(functools.partial(prep_kernel, order, blocks), out_shape=j...]
where the time goes in v2:
time: 79.3 us; the launch traced here: 78.9 us
  blocking collectives  69.5 us (88%)
  Pallas kernels  9.27 us (12%)
    all_to_all x2, blocking collectives, exchange(): lax.all_to_all(value, 'tm', split_axis=0, concat_axis=0, tiled=True, axis...  69.5 us
    pallas_call x1, Pallas kernels, shards(): pl.pallas_call(functools.partial(main_kernel, inner, frames), out_shape=j...  6.37 us
    pallas_call x1, Pallas kernels, shards(): pl.pallas_call(functools.partial(prep_kernel, order, blocks), out_shape=j...  1.7 us

profile of v2, /device:TPU:0, one launch (start us, length us, event | category | flops | bytes accessed | tf_op | source)
XLA Modules:
  0.0 78.9 jit_solution(5155790733250085224)
XLA Ops:
  0.0 1.7 %shard_map.64 = f32[16,144,128]{2,1,0:T(8,128)S(1)} custom-call(f32[8,4,64,128]{3,2,1,0:T(8,128)} %bitcast.10), custom_call_target="tpu_custom_call" | custom-call | tf_op jit(solution)/shard_map/pallas_call | solution.py:373
  1.7 0.0 copy-start
  1.7 0.0 copy-start.1
  1.7 0.0 copy-start.2
  1.7 0.0 copy-start.3
  1.8 0.0 copy-start.4
  1.8 35.9 %all_to_all.10.x_ref = f32[16,144,128]{2,1,0:T(8,128)S(1)} all-to-all(f32[16,144,128]{2,1,0:T(8,128)S(1)} %shard_map.64), channel_id=1, replica_groups={{5,2,7,13,12,11,0,4,8,15,6,14,10,3,9,1},{21,18,23,29,28,27,16,20,24,31,..., dimensions={0} | all-to-all | bytes 2359296 | tf_op jit(solution)/shard_map/all_to_all | solution.py:365
  37.7 0.0 copy-done
  37.7 0.0 copy-done.1
  37.7 0.0 copy-done.2
  37.7 0.0 copy-done.3
  37.7 0.0 copy-done.4
  37.7 6.4 %shard_map.65 = f32[16,160,128]{2,1,0:T(8,128)S(1)} custom-call(f32[16,144,128]{2,1,0:T(8,128)S(1)} %all_to_all.10.x_ref, bf16[4,256,256]{2,1,0:T(8,128)(2,1)S(1)} %copy-done.2, bf16[4,256,256]{2,1,0:T(8,128)(2,1)S(1)} %copy-done.1, bf16[5,256,256]{2,1,0:T(8,128)(2,1)S(1)} %copy-done, f32[16,512]{1,0:T(8,128)S(1)} %copy-done.3, f32[16,512]{1,0:T(8,128)S(1)} %copy-done.4), custom_call_target="tpu_custom_call" | custom-call | tf_op jit(solution)/shard_map/pallas_call | solution.py:403
  44.1 33.6 %all_to_all.11.x_ref = f32[16,160,128]{2,1,0:T(8,128)S(1)} all-to-all(f32[16,160,128]{2,1,0:T(8,128)S(1)} %shard_map.65), channel_id=1, replica_groups={{5,2,7,13,12,11,0,4,8,15,6,14,10,3,9,1},{21,18,23,29,28,27,16,20,24,31,..., dimensions={0} | all-to-all | bytes 2621440 | tf_op jit(solution)/shard_map/all_to_all | solution.py:365
  77.7 1.2 %shard_map.66 = f32[8,4,80,128]{3,2,1,0:T(8,128)} custom-call(f32[16,160,128]{2,1,0:T(8,128)S(1)} %all_to_all.11.x_ref), custom_call_target="tpu_custom_call" | custom-call | tf_op jit(solution)/shard_map/pallas_call | solution.py:424
Async XLA Ops:
  1.7 36.0 %copy-start = (bf16[5,256,256]{2,1,0:T(8,128)(2,1)S(1)}, bf16[5,256,256]{2,1,0:T(8,128)(2,1)}, u32[]{:S(2)}) copy-start(bf16[5,256,256]{2,1,0:T(8,128)(2,1)} %constant.8.clone.res_ref) | copy-start | bytes 1966084
  1.7 36.0 %copy-start.1 = (bf16[4,256,256]{2,1,0:T(8,128)(2,1)S(1)}, bf16[4,256,256]{2,1,0:T(8,128)(2,1)}, u32[]{:S(2)}) copy-start(bf16[4,256,256]{2,1,0:T(8,128)(2,1)} %constant.7.clone.w_lo) | copy-start | bytes 1572868
  1.7 35.9 %copy-start.2 = (bf16[4,256,256]{2,1,0:T(8,128)(2,1)S(1)}, bf16[4,256,256]{2,1,0:T(8,128)(2,1)}, u32[]{:S(2)}) copy-start(bf16[4,256,256]{2,1,0:T(8,128)(2,1)} %constant.6.clone.w_hi) | copy-start | bytes 1572868
  1.7 35.9 %copy-start.3 = (f32[16,512]{1,0:T(8,128)S(1)}, f32[16,512]{1,0:T(8,128)}, u32[]{:S(2)}) copy-start(f32[16,512]{1,0:T(8,128)} %st_ref.1) | copy-start | bytes 98308
  1.8 35.9 %copy-start.4 = (f32[16,512]{1,0:T(8,128)S(1)}, f32[16,512]{1,0:T(8,128)}, u32[]{:S(2)}) copy-start(f32[16,512]{1,0:T(8,128)} %at_ref.1) | copy-start | bytes 98308

commit v3 on v2

--- a/solution.py
+++ b/solution.py
@@ -14,8 +14,10 @@
 UP, DOWN = 5, 4
 LANES = 128
 SUB = 8
-ORDER = [5, 2, 7, 13, 12, 11, 0, 4, 8, 15, 6, 14, 10, 3, 9, 1]
-PREP_VMEM = 8 << 20
+ORDERS = [
+    [9, 3, 7, 13, 12, 8, 0, 4, 1, 15, 6, 14, 10, 2, 5, 11],
+    [9, 10, 3, 13, 5, 12, 11, 0, 4, 1, 15, 6, 14, 7, 2, 8],
+]
 HALO = 32
 
 
@@ -102,12 +104,12 @@
 
 
 def main_kernel(
-    order, frames, x_ref, w_hi, w_lo, res_ref, st_ref, at_ref, o_ref,
+    inputs, order, frames, x_ref, w_hi, w_lo, res_ref, st_ref, at_ref, o_ref,
     a_ref, v_ref, y_ref, yh_ref, yl_ref, z_ref, u_ref, bh_ref, bl_ref,
 ):
     blocks = frames // LANES
-    count = len(order)
-    place_of = {dev: place for place, dev in enumerate(order)}
+    count = len(inputs)
+    place_of = {dev: place for place, dev in enumerate(inputs)}
     f32 = jnp.float32
 
     def dot(a, b):
@@ -133,7 +135,7 @@
 
     total = frames + HALO
 
-    @pl.loop(0, total // 16)
+    @pl.loop(0, total // 16, unroll=3)
     def _(i):
         row = pl.ds(pl.multiple_of(i * 16, 16), 16)
         re = [a_ref[r, row, :LANES] for r in range(4)]
@@ -162,8 +164,7 @@
     groups = (total // 4 - 4 + SUB) // SUB
     for q in range(4):
 
-        @pl.loop(0, groups, unroll=3)
-        def _(t):
+        def step(t, q=q):
             base = t * 32 + 16
             accs = {}
             vals = {}
@@ -185,8 +186,15 @@
                         accs[part, b] = term if p == 0 else accs[part, b] + term
             for part in range(2):
                 for b in range(4):
-                    row = pl.ds(pl.multiple_of(t * SUB, SUB) + SUB, SUB)
+                    row = pl.ds(t * SUB + SUB, SUB) if isinstance(t, int) else pl.ds(pl.multiple_of(t * SUB, SUB) + SUB, SUB)
                     y_ref[part * 16 + b * 4 + q, row, :] = accs[part, b]
+
+        if q == 3:
+            for t in range(groups):
+                step(t)
+        else:
+            pl.loop(0, groups, unroll=3)(step)
+
 
     rows = groups * SUB
     both = 2 * rows
@@ -234,8 +242,7 @@
     groups2 = frames // 4 // SUB
     for q in range(4):
 
-        @pl.loop(0, groups2, unroll=2)
-        def _(t):
+        def step(t, q=q):
             accs = {}
             vals = {}
 
@@ -261,7 +268,14 @@
                     row = pl.ds(t * SUB * UP + g, SUB, stride=UP)
                     u_ref[part * 4 + q, row, :] = accs[part, g]
 
-    @pl.loop(0, outs // 16)
+        if q == 0:
+            for t in range(groups2):
+                step(t)
+        else:
+            pl.loop(0, groups2, unroll=2)(step)
+
+
+    @pl.loop(0, outs // 16, unroll=4)
     def _(i):
         row = pl.ds(pl.multiple_of(i * 16, 16), 16)
         re = [u_ref[q, row, :] for q in range(4)]
@@ -343,15 +357,13 @@
         copy.wait()
 
 
-def shards(order, spectra, synth_taps, analysis_taps):
+def shards(order_in, order_out, spectra, synth_taps, analysis_taps):
     count = lax.axis_size("tm")
     channels, parts, length = spectra.shape
     width = channels * count
     frames = length // count
     outs = frames * UP // DOWN
     blocks = frames // LANES
-    order = tuple(order)
-    groups = [list(order)]
     tiled = channels == 4 * SUB
     vmem = pl.BlockSpec(memory_space=pltpu.VMEM)
     hbm = pl.BlockSpec(memory_space=pltpu.HBM)
@@ -361,9 +373,9 @@
     sub = channels // 4
     small = pltpu.CompilerParams(vmem_limit_bytes=8 << 20)
 
-    def exchange(value):
+    def exchange(value, order):
         return lax.all_to_all(
-            value, "tm", split_axis=0, concat_axis=0, tiled=True, axis_index_groups=groups
+            value, "tm", split_axis=0, concat_axis=0, tiled=True, axis_index_groups=[list(order)]
         )
 
     if tiled:
@@ -371,7 +383,7 @@
         flat = flat.reshape(sub, 4, -1, LANES)
         flat = pltpu.with_memory_space_constraint(flat, pltpu.HBM)
         sent = pl.pallas_call(
-            functools.partial(prep_kernel, order, blocks),
+            functools.partial(prep_kernel, order_in, blocks),
             out_shape=jax.ShapeDtypeStruct((count, rows_in, LANES), f32),
             in_specs=[hbm],
             out_specs=vmem,
@@ -379,30 +391,29 @@
                 pltpu.VMEM((4, sub) + flat.shape[2:], f32),
                 pltpu.SemaphoreType.DMA((4,)),
             ],
-            compiler_params=pltpu.CompilerParams(vmem_limit_bytes=PREP_VMEM),
+            compiler_params=small,
         )(flat)
-        received = exchange(sent)
-        inner = order
+        received = exchange(sent, order_in)
+        inner = (order_in, order_out)
     else:
         cut = spectra.reshape(sub, 4, 2, count, blocks, LANES).transpose(3, 1, 4, 2, 0, 5)
         tail = spectra.reshape(sub, 4, 2, count, frames)[..., frames - HALO :]
         tail = jnp.concatenate([jnp.zeros_like(tail[..., :1, :]), tail[..., :-1, :]], axis=3)
         tail = tail.transpose(3, 2, 0, 1, 4).reshape(count, 2 * sub, LANES)
         sent = jnp.concatenate([cut.reshape(count, 8 * blocks * sub, LANES), tail], axis=1)
-        received = exchange(sent[np.array(order)])
-        received = received[np.argsort(np.array(order))]
+        received = exchange(sent, range(count))
         tiles = 8 * blocks + 2
-        inner = tuple(range(width // 4 // SUB))
+        inner = (range(width // 4 // SUB),) * 2
         received = received.reshape(count, tiles, sub, LANES).transpose(1, 0, 2, 3)
-        received = received.reshape(tiles, len(inner), SUB, LANES).transpose(1, 0, 2, 3)
-        received = received.reshape(len(inner), tiles * SUB, LANES)
+        received = received.reshape(tiles, len(inner[0]), SUB, LANES).transpose(1, 0, 2, 3)
+        received = received.reshape(len(inner[0]), tiles * SUB, LANES)
 
     w_hi, w_lo = radix4_tables(width)
     res = resampler_tables()
     rows = ((frames + HALO) // 4 - 4 + SUB) // SUB * SUB
     made = pl.pallas_call(
-        functools.partial(main_kernel, inner, frames),
-        out_shape=jax.ShapeDtypeStruct((len(inner), rows_out, LANES), f32),
+        functools.partial(main_kernel, *inner, frames),
+        out_shape=jax.ShapeDtypeStruct((len(inner[0]), rows_out, LANES), f32),
         in_specs=[vmem] * 6,
         out_specs=vmem,
         scratch_shapes=[
@@ -420,9 +431,9 @@
     )(received, w_hi, w_lo, res, synth_taps, analysis_taps)
 
     if tiled:
-        back = exchange(made)
+        back = exchange(made, order_out)
         out = pl.pallas_call(
-            functools.partial(final_kernel, order),
+            functools.partial(final_kernel, order_out),
             out_shape=jax.ShapeDtypeStruct((sub, 4, 2 * count * outs // LANES, LANES), f32),
             in_specs=[vmem],
             out_specs=hbm,
@@ -435,10 +446,9 @@
         out = out.reshape(channels, count * outs // LANES, 2, LANES).transpose(0, 2, 1, 3)
         return out.reshape(channels, 2, count * outs)
     tiles = rows_out // SUB
-    made = made.reshape(len(inner), tiles, SUB, LANES).transpose(1, 0, 2, 3)
+    made = made.reshape(len(inner[0]), tiles, SUB, LANES).transpose(1, 0, 2, 3)
     made = made.reshape(tiles, count, sub, LANES).transpose(1, 0, 2, 3)
-    back = exchange(made[np.array(order)])
-    back = back[np.argsort(np.array(order))]
+    back = exchange(made, range(count))
     full = outs // LANES
     head = back[:, : 8 * full].reshape(count, full, 4, 2, sub, LANES).transpose(4, 2, 3, 0, 1, 5)
     head = head.reshape(channels, 2, count, full * LANES)
@@ -450,11 +460,11 @@
 def solution(mesh):
     in_specs = (P("tm", "station", None), P(), P())
     out_specs = P("tm", "station", None)
-    order = list(range(mesh.shape["tm"]))
-    if len(order) == len(ORDER):
-        order = ORDER
+    orders = [list(range(mesh.shape["tm"]))] * 2
+    if len(orders[0]) == len(ORDERS[0]):
+        orders = ORDERS
     return jax.shard_map(
-        functools.partial(shards, order),
+        functools.partial(shards, *orders),
         mesh=mesh,
         in_specs=in_specs,
         out_specs=out_specs,

time: 79.3 us -> 77.3 us (0.975)
  blocking collectives: 69.5 us -> 68 us
    all_to_all x2, blocking collectives: 69.5 us -> 68 us  [exchange(): lax.all_to_all(value, 'tm', split_axis=0, concat_axis=0, tiled=True, axis...]
where the time goes in v3:
time: 77.3 us; the launch traced here: 77.1 us
  blocking collectives  68 us (88%)
  Pallas kernels  8.93 us (12%)
    all_to_all x2, blocking collectives, exchange(): lax.all_to_all(value, 'tm', split_axis=0, concat_axis=0, tiled=True, axis...  68 us
    pallas_call x1, Pallas kernels, shards(): pl.pallas_call(functools.partial(main_kernel, *inner, frames), out_shape=...  6.02 us
    pallas_call x1, Pallas kernels, shards(): pl.pallas_call(functools.partial(prep_kernel, order_in, blocks), out_shap...  1.7 us

profile of v3, /device:TPU:0, one launch (start us, length us, event | category | flops | bytes accessed | tf_op | source)
XLA Modules:
  0.0 77.1 jit_solution(4740586750314351564)
XLA Ops:
  0.0 1.7 %shard_map.64 = f32[16,144,128]{2,1,0:T(8,128)S(1)} custom-call(f32[8,4,64,128]{3,2,1,0:T(8,128)} %bitcast.10), custom_call_target="tpu_custom_call" | custom-call | tf_op jit(solution)/shard_map/pallas_call | solution.py:385
  1.7 0.0 copy-start
  1.7 0.0 copy-start.1
  1.7 0.0 copy-start.2
  1.7 0.0 copy-start.3
  1.8 0.0 copy-start.4
  1.8 35.0 %all_to_all.10.x_ref = f32[16,144,128]{2,1,0:T(8,128)S(1)} all-to-all(f32[16,144,128]{2,1,0:T(8,128)S(1)} %shard_map.64), channel_id=1, replica_groups={{9,3,7,13,12,8,0,4,1,15,6,14,10,2,5,11},{25,19,23,29,28,24,16,20,17,31,..., dimensions={0} | all-to-all | bytes 2359296 | tf_op jit(solution)/shard_map/all_to_all | solution.py:377
  36.7 0.0 copy-done
  36.7 0.0 copy-done.1
  36.7 0.0 copy-done.2
  36.7 0.0 copy-done.3
  36.7 0.0 copy-done.4
  36.8 6.0 %shard_map.65 = f32[16,160,128]{2,1,0:T(8,128)S(1)} custom-call(f32[16,144,128]{2,1,0:T(8,128)S(1)} %all_to_all.10.x_ref, bf16[4,256,256]{2,1,0:T(8,128)(2,1)S(1)} %copy-done.2, bf16[4,256,256]{2,1,0:T(8,128)(2,1)S(1)} %copy-done.1, bf16[5,256,256]{2,1,0:T(8,128)(2,1)S(1)} %copy-done, f32[16,512]{1,0:T(8,128)S(1)} %copy-done.3, f32[16,512]{1,0:T(8,128)S(1)} %copy-done.4), custom_call_target="tpu_custom_call" | custom-call | tf_op jit(solution)/shard_map/pallas_call | solution.py:414
  42.8 33.1 %all_to_all.11.x_ref = f32[16,160,128]{2,1,0:T(8,128)S(1)} all-to-all(f32[16,160,128]{2,1,0:T(8,128)S(1)} %shard_map.65), channel_id=1, replica_groups={{9,10,3,13,5,12,11,0,4,1,15,6,14,7,2,8},{25,26,19,29,21,28,27,16,20,17,..., dimensions={0} | all-to-all | bytes 2621440 | tf_op jit(solution)/shard_map/all_to_all | solution.py:377
  75.8 1.2 %shard_map.66 = f32[8,4,80,128]{3,2,1,0:T(8,128)} custom-call(f32[16,160,128]{2,1,0:T(8,128)S(1)} %all_to_all.11.x_ref), custom_call_target="tpu_custom_call" | custom-call | tf_op jit(solution)/shard_map/pallas_call | solution.py:435
Async XLA Ops:
  1.7 35.0 %copy-start = (bf16[5,256,256]{2,1,0:T(8,128)(2,1)S(1)}, bf16[5,256,256]{2,1,0:T(8,128)(2,1)}, u32[]{:S(2)}) copy-start(bf16[5,256,256]{2,1,0:T(8,128)(2,1)} %constant.8.clone.res_ref) | copy-start | bytes 1966084
  1.7 35.0 %copy-start.1 = (bf16[4,256,256]{2,1,0:T(8,128)(2,1)S(1)}, bf16[4,256,256]{2,1,0:T(8,128)(2,1)}, u32[]{:S(2)}) copy-start(bf16[4,256,256]{2,1,0:T(8,128)(2,1)} %constant.7.clone.w_lo) | copy-start | bytes 1572868
  1.7 35.0 %copy-start.2 = (bf16[4,256,256]{2,1,0:T(8,128)(2,1)S(1)}, bf16[4,256,256]{2,1,0:T(8,128)(2,1)}, u32[]{:S(2)}) copy-start(bf16[4,256,256]{2,1,0:T(8,128)(2,1)} %constant.6.clone.w_hi) | copy-start | bytes 1572868
  1.7 35.0 %copy-start.3 = (f32[16,512]{1,0:T(8,128)S(1)}, f32[16,512]{1,0:T(8,128)}, u32[]{:S(2)}) copy-start(f32[16,512]{1,0:T(8,128)} %st_ref.1) | copy-start | bytes 98308
  1.8 35.0 %copy-start.4 = (f32[16,512]{1,0:T(8,128)S(1)}, f32[16,512]{1,0:T(8,128)}, u32[]{:S(2)}) copy-start(f32[16,512]{1,0:T(8,128)} %at_ref.1) | copy-start | bytes 98308

commit v4 on v3

--- a/solution.py
+++ b/solution.py
@@ -15,8 +15,8 @@
 LANES = 128
 SUB = 8
 ORDERS = [
-    [9, 3, 7, 13, 12, 8, 0, 4, 1, 15, 6, 14, 10, 2, 5, 11],
-    [9, 10, 3, 13, 5, 12, 11, 0, 4, 1, 15, 6, 14, 7, 2, 8],
+    [9, 3, 7, 13, 12, 8, 11, 0, 4, 1, 15, 6, 14, 10, 2, 5],
+    [9, 10, 6, 5, 13, 12, 11, 0, 4, 1, 15, 3, 14, 7, 2, 8],
 ]
 HALO = 32
 
@@ -65,6 +65,10 @@
     return np.stack(out)
 
 
+def pitched(rows):
+    return (rows // SUB // 2 * 2 + 1) * SUB if rows // SUB % 2 == 0 else rows
+
+
 def lane_iota():
     return lax.broadcasted_iota(jnp.int32, (SUB, LANES), 1)
 
@@ -73,20 +77,21 @@
     sub, _, length, _ = x_ref.shape
     lane = lane_iota()
     copies = [
-        pltpu.make_async_copy(x_ref.at[:, r], buf_ref.at[r], sems.at[r]) for r in range(4)
+        pltpu.make_async_copy(x_ref.at[:, r], buf_ref.at[r, :, 0:length], sems.at[r]) for r in range(4)
     ]
     for copy in copies:
         copy.start()
     for r in range(4):
         copies[r].wait()
-        flat_ref = buf_ref.at[r].reshape(sub * length, LANES)
+        pitch = buf_ref.shape[2]
+        flat_ref = buf_ref.at[r].reshape(sub * pitch, LANES)
         for place, dev in enumerate(order):
             for lb in range(blocks):
                 for part in range(2):
                     t = (r * blocks + lb) * 2 + part
                     row = 2 * (blocks * dev + lb) + part
                     o_ref[place, t * SUB : (t + 1) * SUB, :] = flat_ref[
-                        pl.ds(row, SUB, stride=length), :
+                        pl.ds(row, SUB, stride=pitch), :
                     ]
     for place, dev in enumerate(order):
         for part in range(2):
@@ -333,7 +338,8 @@
         return x_ref[place_of[dev], t * SUB : (t + 1) * SUB, :]
 
     for r in range(4):
-        flat_ref = buf_ref.at[r].reshape(SUB * length, LANES)
+        pitch = buf_ref.shape[2]
+        flat_ref = buf_ref.at[r].reshape(SUB * pitch, LANES)
         for dev in range(0, len(order), 2):
             for part in range(2):
                 t = r * 2 + part
@@ -350,8 +356,8 @@
                 ]
                 for k, value in enumerate(values):
                     first = (5 * (dev // 2) + k) * 2 + part
-                    flat_ref[pl.ds(first, SUB, stride=length), :] = value
-        copies.append(pltpu.make_async_copy(buf_ref.at[r], o_ref.at[:, r], sems.at[r]))
+                    flat_ref[pl.ds(first, SUB, stride=pitch), :] = value
+        copies.append(pltpu.make_async_copy(buf_ref.at[r, :, 0:length], o_ref.at[:, r], sems.at[r]))
         copies[-1].start()
     for copy in copies:
         copy.wait()
@@ -388,7 +394,7 @@
             in_specs=[hbm],
             out_specs=vmem,
             scratch_shapes=[
-                pltpu.VMEM((4, sub) + flat.shape[2:], f32),
+                pltpu.VMEM((4, sub, pitched(flat.shape[2]), LANES), f32),
                 pltpu.SemaphoreType.DMA((4,)),
             ],
             compiler_params=small,
@@ -438,7 +444,7 @@
             in_specs=[vmem],
             out_specs=hbm,
             scratch_shapes=[
-                pltpu.VMEM((4, sub, 2 * count * outs // LANES, LANES), f32),
+                pltpu.VMEM((4, sub, pitched(2 * count * outs // LANES), LANES), f32),
                 pltpu.SemaphoreType.DMA((4,)),
             ],
             compiler_params=small,

time: 77.3 us -> 76.7 us (level)
  no operation moved by 1% of the time
where the time goes in v4:
time: 76.7 us; the launch traced here: 76.5 us
  blocking collectives  67.7 us (88%)
  Pallas kernels  8.63 us (11%)
    all_to_all x2, blocking collectives, exchange(): lax.all_to_all(value, 'tm', split_axis=0, concat_axis=0, tiled=True, axis...  67.7 us
    pallas_call x1, Pallas kernels, shards(): pl.pallas_call(functools.partial(main_kernel, *inner, frames), out_shape=...  6.02 us

profile of v4, /device:TPU:0, one launch (start us, length us, event | category | flops | bytes accessed | tf_op | source)
XLA Modules:
  0.0 76.5 jit_solution(6922243858575898069)
XLA Ops:
  0.0 1.4 %shard_map.64 = f32[16,144,128]{2,1,0:T(8,128)S(1)} custom-call(f32[8,4,64,128]{3,2,1,0:T(8,128)} %bitcast.10), custom_call_target="tpu_custom_call" | custom-call | tf_op jit(solution)/shard_map/pallas_call | solution.py:391
  1.4 0.0 copy-start
  1.4 0.0 copy-start.1
  1.4 0.0 copy-start.2
  1.5 0.0 copy-start.3
  1.5 0.0 copy-start.4
  1.5 34.9 %all_to_all.10.x_ref = f32[16,144,128]{2,1,0:T(8,128)S(1)} all-to-all(f32[16,144,128]{2,1,0:T(8,128)S(1)} %shard_map.64), channel_id=1, replica_groups={{9,3,7,13,12,8,11,0,4,1,15,6,14,10,2,5},{25,19,23,29,28,24,27,16,20,17,..., dimensions={0} | all-to-all | bytes 2359296 | tf_op jit(solution)/shard_map/all_to_all | solution.py:383
  36.4 0.0 copy-done
  36.4 0.0 copy-done.1
  36.4 0.0 copy-done.2
  36.4 0.0 copy-done.3
  36.4 0.0 copy-done.4
  36.4 6.0 %shard_map.65 = f32[16,160,128]{2,1,0:T(8,128)S(1)} custom-call(f32[16,144,128]{2,1,0:T(8,128)S(1)} %all_to_all.10.x_ref, bf16[4,256,256]{2,1,0:T(8,128)(2,1)S(1)} %copy-done.2, bf16[4,256,256]{2,1,0:T(8,128)(2,1)S(1)} %copy-done.1, bf16[5,256,256]{2,1,0:T(8,128)(2,1)S(1)} %copy-done, f32[16,512]{1,0:T(8,128)S(1)} %copy-done.3, f32[16,512]{1,0:T(8,128)S(1)} %copy-done.4), custom_call_target="tpu_custom_call" | custom-call | tf_op jit(solution)/shard_map/pallas_call | solution.py:420
  42.5 32.8 %all_to_all.11.x_ref = f32[16,160,128]{2,1,0:T(8,128)S(1)} all-to-all(f32[16,160,128]{2,1,0:T(8,128)S(1)} %shard_map.65), channel_id=1, replica_groups={{9,10,6,5,13,12,11,0,4,1,15,3,14,7,2,8},{25,26,22,21,29,28,27,16,20,17,..., dimensions={0} | all-to-all | bytes 2621440 | tf_op jit(solution)/shard_map/all_to_all | solution.py:383
  75.3 1.2 %shard_map.66 = f32[8,4,80,128]{3,2,1,0:T(8,128)} custom-call(f32[16,160,128]{2,1,0:T(8,128)S(1)} %all_to_all.11.x_ref), custom_call_target="tpu_custom_call" | custom-call | tf_op jit(solution)/shard_map/pallas_call | solution.py:441
Async XLA Ops:
  1.4 35.0 %copy-start = (bf16[5,256,256]{2,1,0:T(8,128)(2,1)S(1)}, bf16[5,256,256]{2,1,0:T(8,128)(2,1)}, u32[]{:S(2)}) copy-start(bf16[5,256,256]{2,1,0:T(8,128)(2,1)} %constant.8.clone.res_ref) | copy-start | bytes 1966084
  1.4 35.0 %copy-start.1 = (bf16[4,256,256]{2,1,0:T(8,128)(2,1)S(1)}, bf16[4,256,256]{2,1,0:T(8,128)(2,1)}, u32[]{:S(2)}) copy-start(bf16[4,256,256]{2,1,0:T(8,128)(2,1)} %constant.7.clone.w_lo) | copy-start | bytes 1572868
  1.4 35.0 %copy-start.2 = (bf16[4,256,256]{2,1,0:T(8,128)(2,1)S(1)}, bf16[4,256,256]{2,1,0:T(8,128)(2,1)}, u32[]{:S(2)}) copy-start(bf16[4,256,256]{2,1,0:T(8,128)(2,1)} %constant.6.clone.w_hi) | copy-start | bytes 1572868
  1.5 35.0 %copy-start.3 = (f32[16,512]{1,0:T(8,128)S(1)}, f32[16,512]{1,0:T(8,128)}, u32[]{:S(2)}) copy-start(f32[16,512]{1,0:T(8,128)} %st_ref.1) | copy-start | bytes 98308
  1.5 34.9 %copy-start.4 = (f32[16,512]{1,0:T(8,128)S(1)}, f32[16,512]{1,0:T(8,128)}, u32[]{:S(2)}) copy-start(f32[16,512]{1,0:T(8,128)} %at_ref.1) | copy-start | bytes 98308

commit v5 on v4

--- a/solution.py
+++ b/solution.py
@@ -16,7 +16,7 @@
 SUB = 8
 ORDERS = [
     [9, 3, 7, 13, 12, 8, 11, 0, 4, 1, 15, 6, 14, 10, 2, 5],
-    [9, 10, 6, 5, 13, 12, 11, 0, 4, 1, 15, 3, 14, 7, 2, 8],
+    [9, 10, 6, 11, 13, 12, 5, 0, 4, 1, 15, 3, 14, 7, 2, 8],
 ]
 HALO = 32
 
@@ -194,7 +194,7 @@
                     row = pl.ds(t * SUB + SUB, SUB) if isinstance(t, int) else pl.ds(pl.multiple_of(t * SUB, SUB) + SUB, SUB)
                     y_ref[part * 16 + b * 4 + q, row, :] = accs[part, b]
 
-        if q == 3:
+        if q >= 2:
             for t in range(groups):
                 step(t)
         else:
@@ -277,7 +277,7 @@
             for t in range(groups2):
                 step(t)
         else:
-            pl.loop(0, groups2, unroll=2)(step)
+            pl.loop(0, groups2, unroll=4)(step)
 
 
     @pl.loop(0, outs // 16, unroll=4)

time: 76.7 us -> 76.5 us (level)
  no operation moved by 1% of the time
where the time goes in v5:
time: 76.5 us; the launch traced here: 76.3 us
  blocking collectives  67.8 us (89%)
  Pallas kernels  8.45 us (11%)
    all_to_all x2, blocking collectives, exchange(): lax.all_to_all(value, 'tm', split_axis=0, concat_axis=0, tiled=True, axis...  67.8 us
    pallas_call x1, Pallas kernels, shards(): pl.pallas_call(functools.partial(main_kernel, *inner, frames), out_shape=...  5.84 us

profile of v5, /device:TPU:0, one launch (start us, length us, event | category | flops | bytes accessed | tf_op | source)
XLA Modules:
  0.0 76.3 jit_solution(1543347897292305602)
XLA Ops:
  0.0 1.4 %shard_map.64 = f32[16,144,128]{2,1,0:T(8,128)S(1)} custom-call(f32[8,4,64,128]{3,2,1,0:T(8,128)} %bitcast.10), custom_call_target="tpu_custom_call" | custom-call | tf_op jit(solution)/shard_map/pallas_call | solution.py:391
  1.4 0.0 copy-start
  1.4 0.0 copy-start.1
  1.4 0.0 copy-start.2
  1.5 0.0 copy-start.3
  1.5 0.0 copy-start.4
  1.5 34.9 %all_to_all.10.x_ref = f32[16,144,128]{2,1,0:T(8,128)S(1)} all-to-all(f32[16,144,128]{2,1,0:T(8,128)S(1)} %shard_map.64), channel_id=1, replica_groups={{9,3,7,13,12,8,11,0,4,1,15,6,14,10,2,5},{25,19,23,29,28,24,27,16,20,17,..., dimensions={0} | all-to-all | bytes 2359296 | tf_op jit(solution)/shard_map/all_to_all | solution.py:383
  36.4 0.0 copy-done
  36.4 0.0 copy-done.1
  36.4 0.0 copy-done.2
  36.4 0.0 copy-done.3
  36.4 0.0 copy-done.4
  36.4 5.8 %shard_map.65 = f32[16,160,128]{2,1,0:T(8,128)S(1)} custom-call(f32[16,144,128]{2,1,0:T(8,128)S(1)} %all_to_all.10.x_ref, bf16[4,256,256]{2,1,0:T(8,128)(2,1)S(1)} %copy-done.2, bf16[4,256,256]{2,1,0:T(8,128)(2,1)S(1)} %copy-done.1, bf16[5,256,256]{2,1,0:T(8,128)(2,1)S(1)} %copy-done, f32[16,512]{1,0:T(8,128)S(1)} %copy-done.3, f32[16,512]{1,0:T(8,128)S(1)} %copy-done.4), custom_call_target="tpu_custom_call" | custom-call | tf_op jit(solution)/shard_map/pallas_call | solution.py:420
  42.3 32.8 %all_to_all.11.x_ref = f32[16,160,128]{2,1,0:T(8,128)S(1)} all-to-all(f32[16,160,128]{2,1,0:T(8,128)S(1)} %shard_map.65), channel_id=1, replica_groups={{9,10,6,11,13,12,5,0,4,1,15,3,14,7,2,8},{25,26,22,27,29,28,21,16,20,17,..., dimensions={0} | all-to-all | bytes 2621440 | tf_op jit(solution)/shard_map/all_to_all | solution.py:383
  75.1 1.2 %shard_map.66 = f32[8,4,80,128]{3,2,1,0:T(8,128)} custom-call(f32[16,160,128]{2,1,0:T(8,128)S(1)} %all_to_all.11.x_ref), custom_call_target="tpu_custom_call" | custom-call | tf_op jit(solution)/shard_map/pallas_call | solution.py:441
Async XLA Ops:
  1.4 35.0 %copy-start = (bf16[5,256,256]{2,1,0:T(8,128)(2,1)S(1)}, bf16[5,256,256]{2,1,0:T(8,128)(2,1)}, u32[]{:S(2)}) copy-start(bf16[5,256,256]{2,1,0:T(8,128)(2,1)} %constant.8.clone.res_ref) | copy-start | bytes 1966084
  1.4 35.0 %copy-start.1 = (bf16[4,256,256]{2,1,0:T(8,128)(2,1)S(1)}, bf16[4,256,256]{2,1,0:T(8,128)(2,1)}, u32[]{:S(2)}) copy-start(bf16[4,256,256]{2,1,0:T(8,128)(2,1)} %constant.7.clone.w_lo) | copy-start | bytes 1572868
  1.4 35.0 %copy-start.2 = (bf16[4,256,256]{2,1,0:T(8,128)(2,1)S(1)}, bf16[4,256,256]{2,1,0:T(8,128)(2,1)}, u32[]{:S(2)}) copy-start(bf16[4,256,256]{2,1,0:T(8,128)(2,1)} %constant.6.clone.w_hi) | copy-start | bytes 1572868
  1.5 35.0 %copy-start.3 = (f32[16,512]{1,0:T(8,128)S(1)}, f32[16,512]{1,0:T(8,128)}, u32[]{:S(2)}) copy-start(f32[16,512]{1,0:T(8,128)} %st_ref.1) | copy-start | bytes 98308
  1.5 34.9 %copy-start.4 = (f32[16,512]{1,0:T(8,128)S(1)}, f32[16,512]{1,0:T(8,128)}, u32[]{:S(2)}) copy-start(f32[16,512]{1,0:T(8,128)} %at_ref.1) | copy-start | bytes 98308

commit v6 on v5

--- a/solution.py
+++ b/solution.py
@@ -16,7 +16,7 @@
 SUB = 8
 ORDERS = [
     [9, 3, 7, 13, 12, 8, 11, 0, 4, 1, 15, 6, 14, 10, 2, 5],
-    [9, 10, 6, 11, 13, 12, 5, 0, 4, 1, 15, 3, 14, 7, 2, 8],
+    [9, 10, 6, 5, 13, 12, 11, 0, 4, 1, 15, 3, 14, 7, 2, 8],
 ]
 HALO = 32
 

time: 76.5 us -> 76.5 us (level)
  no operation moved by 1% of the time
where the time goes in v6:
time: 76.5 us; the launch traced here: 76.3 us
  blocking collectives  67.7 us (88%)
  Pallas kernels  8.45 us (11%)
    all_to_all x2, blocking collectives, exchange(): lax.all_to_all(value, 'tm', split_axis=0, concat_axis=0, tiled=True, axis...  67.7 us
    pallas_call x1, Pallas kernels, shards(): pl.pallas_call(functools.partial(main_kernel, *inner, frames), out_shape=...  5.84 us

profile of v6, /device:TPU:0, one launch (start us, length us, event | category | flops | bytes accessed | tf_op | source)
XLA Modules:
  0.0 76.3 jit_solution(10209813804642362430)
XLA Ops:
  0.0 1.4 %shard_map.64 = f32[16,144,128]{2,1,0:T(8,128)S(1)} custom-call(f32[8,4,64,128]{3,2,1,0:T(8,128)} %bitcast.10), custom_call_target="tpu_custom_call" | custom-call | tf_op jit(solution)/shard_map/pallas_call | solution.py:391
  1.4 0.0 copy-start
  1.4 0.0 copy-start.1
  1.4 0.0 copy-start.2
  1.5 0.0 copy-start.3
  1.5 0.0 copy-start.4
  1.5 34.9 %all_to_all.10.x_ref = f32[16,144,128]{2,1,0:T(8,128)S(1)} all-to-all(f32[16,144,128]{2,1,0:T(8,128)S(1)} %shard_map.64), channel_id=1, replica_groups={{9,3,7,13,12,8,11,0,4,1,15,6,14,10,2,5},{25,19,23,29,28,24,27,16,20,17,..., dimensions={0} | all-to-all | bytes 2359296 | tf_op jit(solution)/shard_map/all_to_all | solution.py:383
  36.4 0.0 copy-done
  36.4 0.0 copy-done.1
  36.4 0.0 copy-done.2
  36.4 0.0 copy-done.3
  36.4 0.0 copy-done.4
  36.4 5.8 %shard_map.65 = f32[16,160,128]{2,1,0:T(8,128)S(1)} custom-call(f32[16,144,128]{2,1,0:T(8,128)S(1)} %all_to_all.10.x_ref, bf16[4,256,256]{2,1,0:T(8,128)(2,1)S(1)} %copy-done.2, bf16[4,256,256]{2,1,0:T(8,128)(2,1)S(1)} %copy-done.1, bf16[5,256,256]{2,1,0:T(8,128)(2,1)S(1)} %copy-done, f32[16,512]{1,0:T(8,128)S(1)} %copy-done.3, f32[16,512]{1,0:T(8,128)S(1)} %copy-done.4), custom_call_target="tpu_custom_call" | custom-call | tf_op jit(solution)/shard_map/pallas_call | solution.py:420
  42.3 32.8 %all_to_all.11.x_ref = f32[16,160,128]{2,1,0:T(8,128)S(1)} all-to-all(f32[16,160,128]{2,1,0:T(8,128)S(1)} %shard_map.65), channel_id=1, replica_groups={{9,10,6,5,13,12,11,0,4,1,15,3,14,7,2,8},{25,26,22,21,29,28,27,16,20,17,..., dimensions={0} | all-to-all | bytes 2621440 | tf_op jit(solution)/shard_map/all_to_all | solution.py:383
  75.1 1.2 %shard_map.66 = f32[8,4,80,128]{3,2,1,0:T(8,128)} custom-call(f32[16,160,128]{2,1,0:T(8,128)S(1)} %all_to_all.11.x_ref), custom_call_target="tpu_custom_call" | custom-call | tf_op jit(solution)/shard_map/pallas_call | solution.py:441
Async XLA Ops:
  1.4 35.0 %copy-start = (bf16[5,256,256]{2,1,0:T(8,128)(2,1)S(1)}, bf16[5,256,256]{2,1,0:T(8,128)(2,1)}, u32[]{:S(2)}) copy-start(bf16[5,256,256]{2,1,0:T(8,128)(2,1)} %constant.8.clone.res_ref) | copy-start | bytes 1966084
  1.4 35.0 %copy-start.1 = (bf16[4,256,256]{2,1,0:T(8,128)(2,1)S(1)}, bf16[4,256,256]{2,1,0:T(8,128)(2,1)}, u32[]{:S(2)}) copy-start(bf16[4,256,256]{2,1,0:T(8,128)(2,1)} %constant.7.clone.w_lo) | copy-start | bytes 1572868
  1.4 35.0 %copy-start.2 = (bf16[4,256,256]{2,1,0:T(8,128)(2,1)S(1)}, bf16[4,256,256]{2,1,0:T(8,128)(2,1)}, u32[]{:S(2)}) copy-start(bf16[4,256,256]{2,1,0:T(8,128)(2,1)} %constant.6.clone.w_hi) | copy-start | bytes 1572868
  1.5 35.0 %copy-start.3 = (f32[16,512]{1,0:T(8,128)S(1)}, f32[16,512]{1,0:T(8,128)}, u32[]{:S(2)}) copy-start(f32[16,512]{1,0:T(8,128)} %st_ref.1) | copy-start | bytes 98308
  1.5 34.9 %copy-start.4 = (f32[16,512]{1,0:T(8,128)S(1)}, f32[16,512]{1,0:T(8,128)}, u32[]{:S(2)}) copy-start(f32[16,512]{1,0:T(8,128)} %at_ref.1) | copy-start | bytes 98308

commit v7 on v6

--- a/solution.py
+++ b/solution.py
@@ -194,7 +194,7 @@
                     row = pl.ds(t * SUB + SUB, SUB) if isinstance(t, int) else pl.ds(pl.multiple_of(t * SUB, SUB) + SUB, SUB)
                     y_ref[part * 16 + b * 4 + q, row, :] = accs[part, b]
 
-        if q >= 2:
+        if q >= 1:
             for t in range(groups):
                 step(t)
         else:

time: 76.5 us -> 76.6 us (level)
  no operation moved by 1% of the time
where the time goes in v7:
time: 76.6 us; the launch traced here: 76.3 us
  blocking collectives  67.7 us (88%)
  Pallas kernels  8.49 us (11%)
    all_to_all x2, blocking collectives, exchange(): lax.all_to_all(value, 'tm', split_axis=0, concat_axis=0, tiled=True, axis...  67.7 us
    pallas_call x1, Pallas kernels, shards(): pl.pallas_call(functools.partial(main_kernel, *inner, frames), out_shape=...  5.88 us

profile of v7, /device:TPU:0, one launch (start us, length us, event | category | flops | bytes accessed | tf_op | source)
XLA Modules:
  0.0 76.3 jit_solution(10760164283346226811)
XLA Ops:
  0.0 1.4 %shard_map.64 = f32[16,144,128]{2,1,0:T(8,128)S(1)} custom-call(f32[8,4,64,128]{3,2,1,0:T(8,128)} %bitcast.10), custom_call_target="tpu_custom_call" | custom-call | tf_op jit(solution)/shard_map/pallas_call | solution.py:391
  1.4 0.0 copy-start
  1.4 0.0 copy-start.1
  1.4 0.0 copy-start.2
  1.5 0.0 copy-start.3
  1.5 0.0 copy-start.4
  1.5 34.9 %all_to_all.10.x_ref = f32[16,144,128]{2,1,0:T(8,128)S(1)} all-to-all(f32[16,144,128]{2,1,0:T(8,128)S(1)} %shard_map.64), channel_id=1, replica_groups={{9,3,7,13,12,8,11,0,4,1,15,6,14,10,2,5},{25,19,23,29,28,24,27,16,20,17,..., dimensions={0} | all-to-all | bytes 2359296 | tf_op jit(solution)/shard_map/all_to_all | solution.py:383
  36.4 0.0 copy-done
  36.4 0.0 copy-done.1
  36.4 0.0 copy-done.2
  36.4 0.0 copy-done.3
  36.4 0.0 copy-done.4
  36.4 5.9 %shard_map.65 = f32[16,160,128]{2,1,0:T(8,128)S(1)} custom-call(f32[16,144,128]{2,1,0:T(8,128)S(1)} %all_to_all.10.x_ref, bf16[4,256,256]{2,1,0:T(8,128)(2,1)S(1)} %copy-done.2, bf16[4,256,256]{2,1,0:T(8,128)(2,1)S(1)} %copy-done.1, bf16[5,256,256]{2,1,0:T(8,128)(2,1)S(1)} %copy-done, f32[16,512]{1,0:T(8,128)S(1)} %copy-done.3, f32[16,512]{1,0:T(8,128)S(1)} %copy-done.4), custom_call_target="tpu_custom_call" | custom-call | tf_op jit(solution)/shard_map/pallas_call | solution.py:420
  42.3 32.8 %all_to_all.11.x_ref = f32[16,160,128]{2,1,0:T(8,128)S(1)} all-to-all(f32[16,160,128]{2,1,0:T(8,128)S(1)} %shard_map.65), channel_id=1, replica_groups={{9,10,6,5,13,12,11,0,4,1,15,3,14,7,2,8},{25,26,22,21,29,28,27,16,20,17,..., dimensions={0} | all-to-all | bytes 2621440 | tf_op jit(solution)/shard_map/all_to_all | solution.py:383
  75.1 1.2 %shard_map.66 = f32[8,4,80,128]{3,2,1,0:T(8,128)} custom-call(f32[16,160,128]{2,1,0:T(8,128)S(1)} %all_to_all.11.x_ref), custom_call_target="tpu_custom_call" | custom-call | tf_op jit(solution)/shard_map/pallas_call | solution.py:441
Async XLA Ops:
  1.4 35.0 %copy-start = (bf16[5,256,256]{2,1,0:T(8,128)(2,1)S(1)}, bf16[5,256,256]{2,1,0:T(8,128)(2,1)}, u32[]{:S(2)}) copy-start(bf16[5,256,256]{2,1,0:T(8,128)(2,1)} %constant.8.clone.res_ref) | copy-start | bytes 1966084
  1.4 35.0 %copy-start.1 = (bf16[4,256,256]{2,1,0:T(8,128)(2,1)S(1)}, bf16[4,256,256]{2,1,0:T(8,128)(2,1)}, u32[]{:S(2)}) copy-start(bf16[4,256,256]{2,1,0:T(8,128)(2,1)} %constant.7.clone.w_lo) | copy-start | bytes 1572868
  1.4 35.0 %copy-start.2 = (bf16[4,256,256]{2,1,0:T(8,128)(2,1)S(1)}, bf16[4,256,256]{2,1,0:T(8,128)(2,1)}, u32[]{:S(2)}) copy-start(bf16[4,256,256]{2,1,0:T(8,128)(2,1)} %constant.6.clone.w_hi) | copy-start | bytes 1572868
  1.5 35.0 %copy-start.3 = (f32[16,512]{1,0:T(8,128)S(1)}, f32[16,512]{1,0:T(8,128)}, u32[]{:S(2)}) copy-start(f32[16,512]{1,0:T(8,128)} %st_ref.1) | copy-start | bytes 98308
  1.5 34.9 %copy-start.4 = (f32[16,512]{1,0:T(8,128)S(1)}, f32[16,512]{1,0:T(8,128)}, u32[]{:S(2)}) copy-start(f32[16,512]{1,0:T(8,128)} %at_ref.1) | copy-start | bytes 98308
